TPU v7x, 32 devices: a whole 2x2x4 slice. The times are simulated.
32 devices in a mesh: slides: 2 (over x), rows: 8 (over z, y), cols: 2 (over core).
Axes of the slice: x: 2, y: 2, z: 4, core: 2. Of those that a mesh axis runs over, the one named last changes fastest.
Arguments:
- image: bfloat16 [512, 512, 128], P(('slides', 'rows'), 'cols'), parts along dimension 0, may hold values from -6 to 6
- tissue: int32 [16, 16], P(('slides', 'rows'), 'cols'), parts along dimension 0, may hold values 0 or 1
- first_kernel: bfloat16 [3, 3, 128, 128], replicated, may hold values from -0.1875 to 0.1875
- first_bias: float32 [128], replicated, may hold values from -3 to 3
- second_kernel: bfloat16 [3, 3, 128, 128], replicated, may hold values from -0.1875 to 0.1875
- second_bias: float32 [128], replicated, may hold values from -3 to 3
Outputs:
- features: bfloat16 [512, 512, 128], P(('slides', 'rows'), 'cols'), parts along dimension 0
There are 2 independent parts, one for each index of `slides`. A program takes and returns all parts, laid end to end along the dimension named above; an argument that names none is the same for every part. Nothing has to cross between parts.
All inputs are finite; a program needn't handle non-finite values. No bound on the sum of `tissue` on one device may be relied on, other than what follows from the above.
Results may differ from a plain program's by a relative error of at most 0.0043.
Values may be sent and summed in bfloat16 or wider, within the bound.
A program may use at most 128 MiB of HBM per device.

v0:
```python
import jax
import jax.numpy as jnp
from jax import lax
from jax.sharding import PartitionSpec as P

MB = 32


def with_halo(value, sides, width):
    for axis, dim in sides:
        peers, length = (lax.axis_size(axis), value.shape[dim])
        up = [(i, (i + 1) % peers) for i in range(peers - 1)]
        down = [(j, i) for i, j in up]
        last = lax.slice_in_dim(value, length - width, length, axis=dim)
        leading = lax.slice_in_dim(value, 0, width, axis=dim)
        before = lax.ppermute(last, axis, up)
        after = lax.ppermute(leading, axis, down)
        value = jnp.concatenate([before, value, after], axis=dim)
    return value


def conv_valid(padded, kernel, bias):
    rows = padded.shape[0] - 2
    cols = padded.shape[1] - 2
    chans = padded.shape[2]
    wide = jnp.concatenate(
        [padded[:, 0:cols], padded[:, 1 : cols + 1], padded[:, 2 : cols + 2]], axis=-1
    )
    total = jnp.zeros((rows * cols, kernel.shape[3]), jnp.float32)
    for offset in range(3):
        block = wide[offset : offset + rows].reshape(rows * cols, 3 * chans)
        total = total + jnp.dot(
            block,
            kernel[offset].reshape(3 * chans, kernel.shape[3]),
            preferred_element_type=jnp.float32,
        )
    return total.reshape(rows, cols, kernel.shape[3]) + bias


def shards(image, tissue, first_kernel, first_bias, second_kernel, second_bias):
    pixel_mask = jnp.repeat(jnp.repeat(tissue, MB, axis=0), MB, axis=1).astype(jnp.float32)[
        :, :, None
    ]
    padded = with_halo(image, (("rows", 0), ("cols", 1)), 1)
    hidden = (jnp.maximum(conv_valid(padded, first_kernel, first_bias), 0.0) * pixel_mask).astype(
        jnp.bfloat16
    )
    widened = with_halo(hidden, (("rows", 0), ("cols", 1)), 1)
    result = conv_valid(widened, second_kernel, second_bias)
    return (jnp.maximum(result, 0.0) * pixel_mask).astype(jnp.bfloat16)


def solution(mesh):
    in_specs = (
        P(("slides", "rows"), "cols", None),
        P(("slides", "rows"), "cols"),
        P(),
        P(),
        P(),
        P(),
    )
    out_specs = P(("slides", "rows"), "cols", None)
    return jax.shard_map(shards, mesh=mesh, in_specs=in_specs, out_specs=out_specs, check_vma=False)
```

profile of v0, /device:TPU:0, one launch (start us, length us, event | category | flops | bytes accessed | tf_op | source)
XLA Modules:
  0.0 72.1 jit_solution(6908949565668198928)
XLA Ops:
  0.0 0.9 %fusion.8 = (bf16[1,256,128]{2,1,0:T(8,128)(2,1)S(1)}, bf16[1,256,128]{2,1,0:T(8,128)(2,1)S(1)}) fusion(bf16[32,256,128]{2,1,0:T(8,128)(2,1)} %param.6), kind=kLoop, calls=%fused_computation.29 | loop fusion | bytes 262144 | tf_op jit(solution)/shard_map/slice | solution.py:15
  0.9 4.9 %collective-permute-start = (bf16[1,256,128]{2,1,0:T(8,128)(2,1)S(1)}, bf16[1,256,128]{2,1,0:T(8,128)(2,1)S(1)}, u32[]{:S(2)}, u32[]{:S(2)}) collective-permute-start(bf16[1,256,128]{2,1,0:T(8,128)(2,1)S(1)} %get-tuple-element.18), channel_id=1, source_target_pairs={{0,2},{2,4},{4,6},{6,8},{8,10},{10,12},{12,14},{1,3},{3,5},{5,7},{... | collective-permute-start | bytes 196616 | tf_op jit(solution)/shard_map/ppermute | solution.py:16
  5.8 1.3 %collective-permute-start.1 = (bf16[1,256,128]{2,1,0:T(8,128)(2,1)S(1)}, bf16[1,256,128]{2,1,0:T(8,128)(2,1)S(1)}, u32[]{:S(2)}, u32[]{:S(2)}) collective-permute-start(bf16[1,256,128]{2,1,0:T(8,128)(2,1)S(1)} %get-tuple-element.17), channel_id=1, source_target_pairs={{2,0},{4,2},{6,4},{8,6},{10,8},{12,10},{14,12},{3,1},{5,3},{7,5},{... | collective-permute-start | bytes 196616 | tf_op jit(solution)/shard_map/ppermute | solution.py:17
  7.1 1.0 %fusion.10 = (bf16[1,3,128,128]{3,2,1,0:T(8,128)(2,1)S(1)}, bf16[1,3,128,128]{3,2,1,0:T(8,128)(2,1)S(1)}, bf16[1,3,128,128]{3,2,1,0:T(8,128)(2,1)S(1)}) fusion(bf16[3,3,128,128]{3,2,1,0:T(8,128)(2,1)} %param.8), kind=kLoop, calls=%fused_computation.31 | loop fusion | bytes 589824 | tf_op jit(solution)/shard_map/slice | solution.py:34
  8.1 0.0 collective-permute-done
  8.1 1.9 %constant_dynamic-update-slice_fusion.1 = bf16[34,256,128]{2,1,0:T(8,128)(2,1)S(1)} fusion(bf16[34,256,128]{2,1,0:T(8,128)(2,1)S(1)} %constant_dynamic-update-slice_fusion.2, bf16[32,256,128]{2,1,0:T(8,128)(2,1)} %param.6), kind=kLoop, calls=%fused_computation.22 | loop fusion | bytes 4194304
  10.1 1.9 %collective-permute-done.1 = bf16[1,256,128]{2,1,0:T(8,128)(2,1)S(1)} collective-permute-done((bf16[1,256,128]{2,1,0:T(8,128)(2,1)S(1)}, bf16[1,256,128]{2,1,0:T(8,128)(2,1)S(1)}, u32[]{:S(2)}, u32[]{:S(2)}) %collective-permute-start.1) | collective-permute-done | bytes 65568 | tf_op jit(solution)/shard_map/ppermute | solution.py:17
  12.0 1.3 %collective-permute-start.2 = (bf16[34,1,128]{2,1,0:T(2,128)(2,1)S(1)}, bf16[34,1,128]{2,1,0:T(2,128)(2,1)S(1)}, u32[]{:S(2)}, u32[]{:S(2)}) collective-permute-start(bf16[34,1,128]{2,1,0:T(2,128)(2,1)S(1)} %get-tuple-element.13), channel_id=1, source_target_pairs={{0,1},{2,3},{4,5},{6,7},{8,9},{10,11},{12,13},{14,15},{16,17},{18,... | collective-permute-start | bytes 26120 | tf_op jit(solution)/shard_map/ppermute | solution.py:16
  13.3 1.3 %collective-permute-start.3 = (bf16[34,1,128]{2,1,0:T(2,128)(2,1)S(1)}, bf16[34,1,128]{2,1,0:T(2,128)(2,1)S(1)}, u32[]{:S(2)}, u32[]{:S(2)}) collective-permute-start(bf16[34,1,128]{2,1,0:T(2,128)(2,1)S(1)} %get-tuple-element.14), channel_id=1, source_target_pairs={{1,0},{3,2},{5,4},{7,6},{9,8},{11,10},{13,12},{15,14},{17,16},{19,... | collective-permute-start | bytes 26120 | tf_op jit(solution)/shard_map/ppermute | solution.py:17
  14.6 0.7 convert_bitcast_fusion
  15.3 0.1 broadcast_in_dim.2
  15.3 0.1 convert_element_type.20
  15.4 0.0 collective-permute-done.2
  15.4 1.0 %collective-permute-done.3 = bf16[34,1,128]{2,1,0:T(2,128)(2,1)S(1)} collective-permute-done((bf16[34,1,128]{2,1,0:T(2,128)(2,1)S(1)}, bf16[34,1,128]{2,1,0:T(2,128)(2,1)S(1)}, u32[]{:S(2)}, u32[]{:S(2)}) %collective-permute-start.3) | collective-permute-done | bytes 8736 | tf_op jit(solution)/shard_map/ppermute | solution.py:17
  16.4 4.5 %fusion.2 = bf16[34,256,384]{2,1,0:T(8,128)(2,1)S(1)} fusion(bf16[34,1,128]{2,1,0:T(2,128)(2,1)S(1)} %collective-permute-done.3, bf16[34,256,128]{2,1,0:T(8,128)(2,1)S(1)} %constant_dynamic-update-slice_fusion, bf16[34,1,128]{2,1,0:T(2,128)(2,1)S(1)} %collective-permute-done.2), kind=kLoop, calls=%fused_computation.13 | loop fusion | flops 33423360 | bytes 8930304 | tf_op jit(solution)/shard_map/concatenate | solution.py:26
  20.9 6.3 %fusion.5 = (bf16[32,256,384]{2,1,0:T(8,128)(2,1)S(1)}, bf16[32,256,384]{2,1,0:T(8,128)(2,1)S(1)}, bf16[32,256,384]{2,1,0:T(8,128)(2,1)S(1)}) fusion(bf16[34,256,384]{2,1,0:T(8,128)(2,1)S(1)} %fusion.2), kind=kLoop, calls=%fused_computation.26 | loop fusion | bytes 37748736 | tf_op jit(solution)/shard_map/slice | solution.py:31
  27.1 1.8 %fusion.11 = f32[8192,128]{1,0:T(8,128)S(1)} fusion(bf16[8192,384]{1,0:T(8,128)(2,1)S(1)} %bitcast.32, bf16[384,128]{1,0:T(8,128)(2,1)S(1)} %bitcast.38), kind=kOutput, calls=%fused_computation.32 | convolution fusion | flops 805306368 | bytes 10584064 | tf_op jit(solution)/shard_map/dot_general | solution.py:32
  28.9 1.8 %convolution_add_fusion.3 = f32[8192,128]{1,0:T(8,128)S(1)} fusion(f32[8192,128]{1,0:T(8,128)S(1)} %fusion.11, bf16[8192,384]{1,0:T(8,128)(2,1)S(1)} %bitcast.30, bf16[384,128]{1,0:T(8,128)(2,1)S(1)} %bitcast.37), kind=kOutput, calls=%fused_computation.3 | convolution fusion | flops 806354944 | bytes 14778368 | tf_op jit(solution)/shard_map/dot_general | solution.py:32
  30.7 0.0 copy-start.1
  30.7 1.8 %convolution_add_fusion.2 = f32[8192,128]{1,0:T(8,128)S(1)} fusion(f32[8192,128]{1,0:T(8,128)S(1)} %convolution_add_fusion.3, bf16[8192,384]{1,0:T(8,128)(2,1)S(1)} %bitcast.28, bf16[384,128]{1,0:T(8,128)(2,1)S(1)} %bitcast.36), kind=kOutput, calls=%fused_computation.2 | convolution fusion | flops 806354944 | bytes 14778368 | tf_op jit(solution)/shard_map/dot_general | solution.py:32
  32.6 0.0 copy-start
  32.6 0.0 copy-done.1
  32.6 0.7 %multiply_convert_fusion.1 = bf16[32,256,128]{2,1,0:T(8,128)(2,1)S(1)} fusion(f32[32,256,128]{2,1,0:T(8,128)S(1)} %bitcast.35, f32[256]{0:T(256)S(1)} %convert_element_type.20, f32[128]{0:T(128)S(1)} %copy-done.1), kind=kLoop, calls=%fused_computation.17 | loop fusion | flops 4194304 | bytes 6292992 | tf_op jit(solution)/shard_map/convert_element_type | solution.py:45
  33.3 4.3 %collective-permute-start.4 = (bf16[1,256,128]{2,1,0:T(8,128)(2,1)S(1)}, bf16[1,256,128]{2,1,0:T(8,128)(2,1)S(1)}, u32[]{:S(2)}, u32[]{:S(2)}) collective-permute-start(bf16[1,256,128]{2,1,0:T(8,128)(2,1)S(1)} %get-tuple-element.15), channel_id=1, source_target_pairs={{0,2},{2,4},{4,6},{6,8},{8,10},{10,12},{12,14},{1,3},{3,5},{5,7},{... | collective-permute-start | bytes 196616 | tf_op jit(solution)/shard_map/ppermute | solution.py:16
  37.7 1.3 %collective-permute-start.5 = (bf16[1,256,128]{2,1,0:T(8,128)(2,1)S(1)}, bf16[1,256,128]{2,1,0:T(8,128)(2,1)S(1)}, u32[]{:S(2)}, u32[]{:S(2)}) collective-permute-start(bf16[1,256,128]{2,1,0:T(8,128)(2,1)S(1)} %get-tuple-element.16), channel_id=1, source_target_pairs={{2,0},{4,2},{6,4},{8,6},{10,8},{12,10},{14,12},{3,1},{5,3},{7,5},{... | collective-permute-start | bytes 196616 | tf_op jit(solution)/shard_map/ppermute | solution.py:17
  39.0 0.6 collective-permute-done.4
  39.6 4.3 %collective-permute-done.5 = bf16[1,256,128]{2,1,0:T(8,128)(2,1)S(1)} collective-permute-done((bf16[1,256,128]{2,1,0:T(8,128)(2,1)S(1)}, bf16[1,256,128]{2,1,0:T(8,128)(2,1)S(1)}, u32[]{:S(2)}, u32[]{:S(2)}) %collective-permute-start.5) | collective-permute-done | bytes 65568 | tf_op jit(solution)/shard_map/ppermute | solution.py:17
  43.9 1.3 %collective-permute-start.6 = (bf16[34,1,128]{2,1,0:T(2,128)(2,1)S(1)}, bf16[34,1,128]{2,1,0:T(2,128)(2,1)S(1)}, u32[]{:S(2)}, u32[]{:S(2)}) collective-permute-start(bf16[34,1,128]{2,1,0:T(2,128)(2,1)S(1)} %get-tuple-element.11), channel_id=1, source_target_pairs={{0,1},{2,3},{4,5},{6,7},{8,9},{10,11},{12,13},{14,15},{16,17},{18,... | collective-permute-start | bytes 26120 | tf_op jit(solution)/shard_map/ppermute | solution.py:16
  45.2 1.5 %collective-permute-start.7 = (bf16[34,1,128]{2,1,0:T(2,128)(2,1)S(1)}, bf16[34,1,128]{2,1,0:T(2,128)(2,1)S(1)}, u32[]{:S(2)}, u32[]{:S(2)}) collective-permute-start(bf16[34,1,128]{2,1,0:T(2,128)(2,1)S(1)} %get-tuple-element.12), channel_id=1, source_target_pairs={{1,0},{3,2},{5,4},{7,6},{9,8},{11,10},{13,12},{15,14},{17,16},{19,... | collective-permute-start | bytes 26120 | tf_op jit(solution)/shard_map/ppermute | solution.py:17
  46.6 0.0 copy-done
  46.7 0.0 collective-permute-done.6
  46.7 1.5 %collective-permute-done.7 = bf16[34,1,128]{2,1,0:T(2,128)(2,1)S(1)} collective-permute-done((bf16[34,1,128]{2,1,0:T(2,128)(2,1)S(1)}, bf16[34,1,128]{2,1,0:T(2,128)(2,1)S(1)}, u32[]{:S(2)}, u32[]{:S(2)}) %collective-permute-start.7) | collective-permute-done | bytes 8736 | tf_op jit(solution)/shard_map/ppermute | solution.py:17
  48.2 10.2 %fusion = bf16[34,256,384]{2,1,0:T(8,128)(2,1)S(1)} fusion(bf16[34,1,128]{2,1,0:T(2,128)(2,1)S(1)} %collective-permute-done.7, bf16[1,256,128]{2,1,0:T(8,128)(2,1)S(1)} %collective-permute-done.5, bf16[32,256,128]{2,1,0:T(8,128)(2,1)S(1)} %multiply_convert_fusion.1, bf16[1,256,128]{2,1,0:T(8,128)(2,1)S(1)} %collective-permute-done.4, ...), kind=kLoop, calls=%fused_computation.5 | loop fusion | flops 73531392 | bytes 8930304 | tf_op jit(solution)/shard_map/concatenate | solution.py:26
  58.4 6.3 %fusion.4 = (bf16[32,256,384]{2,1,0:T(8,128)(2,1)S(1)}, bf16[32,256,384]{2,1,0:T(8,128)(2,1)S(1)}, bf16[32,256,384]{2,1,0:T(8,128)(2,1)S(1)}) fusion(bf16[34,256,384]{2,1,0:T(8,128)(2,1)S(1)} %fusion), kind=kLoop, calls=%fused_computation.25 | loop fusion | bytes 37748736 | tf_op jit(solution)/shard_map/slice | solution.py:31
  64.7 1.8 %fusion.12 = f32[8192,128]{1,0:T(8,128)S(1)} fusion(bf16[8192,384]{1,0:T(8,128)(2,1)S(1)} %bitcast.33, bf16[384,128]{1,0:T(8,128)(2,1)S(1)} %bitcast.41), kind=kOutput, calls=%fused_computation.33 | convolution fusion | flops 805306368 | bytes 10584064 | tf_op jit(solution)/shard_map/dot_general | solution.py:32
  66.5 1.8 %convolution_add_fusion.1 = f32[8192,128]{1,0:T(8,128)S(1)} fusion(f32[8192,128]{1,0:T(8,128)S(1)} %fusion.12, bf16[8192,384]{1,0:T(8,128)(2,1)S(1)} %bitcast.31, bf16[384,128]{1,0:T(8,128)(2,1)S(1)} %bitcast.40), kind=kOutput, calls=%fused_computation.1 | convolution fusion | flops 806354944 | bytes 14778368 | tf_op jit(solution)/shard_map/dot_general | solution.py:32
  68.3 0.0 copy-start.2
  68.3 1.8 %convolution_add_fusion = f32[8192,128]{1,0:T(8,128)S(1)} fusion(f32[8192,128]{1,0:T(8,128)S(1)} %convolution_add_fusion.1, bf16[8192,384]{1,0:T(8,128)(2,1)S(1)} %bitcast.29, bf16[384,128]{1,0:T(8,128)(2,1)S(1)} %bitcast.39), kind=kOutput, calls=%fused_computation | convolution fusion | flops 806354944 | bytes 14778368 | tf_op jit(solution)/shard_map/dot_general | solution.py:32
  70.1 0.0 copy-done.2
  70.1 2.0 %multiply_convert_fusion = bf16[32,256,128]{2,1,0:T(8,128)(2,1)} fusion(f32[32,256,128]{2,1,0:T(8,128)S(1)} %bitcast.34, f32[128]{0:T(128)S(1)} %copy-done.2, f32[256]{0:T(256)S(1)} %convert_element_type.20), kind=kLoop, calls=%fused_computation.16 | loop fusion | flops 4194304 | bytes 6292992 | tf_op jit(solution)/shard_map/convert_element_type | solution.py:50
  (6 shorter events, 0.1 us)
Async XLA Ops:
  0.9 7.2 %collective-permute-start = (bf16[1,256,128]{2,1,0:T(8,128)(2,1)S(1)}, bf16[1,256,128]{2,1,0:T(8,128)(2,1)S(1)}, u32[]{:S(2)}, u32[]{:S(2)}) collective-permute-start(bf16[1,256,128]{2,1,0:T(8,128)(2,1)S(1)} %get-tuple-element.18), channel_id=1, source_target_pairs={{0,2},{2,4},{4,6},{6,8},{8,10},{10,12},{12,14},{1,3},{3,5},{5,7},{... | collective-permute-start | bytes 196616 | tf_op jit(solution)/shard_map/ppermute | solution.py:16
  5.8 6.2 %collective-permute-start.1 = (bf16[1,256,128]{2,1,0:T(8,128)(2,1)S(1)}, bf16[1,256,128]{2,1,0:T(8,128)(2,1)S(1)}, u32[]{:S(2)}, u32[]{:S(2)}) collective-permute-start(bf16[1,256,128]{2,1,0:T(8,128)(2,1)S(1)} %get-tuple-element.17), channel_id=1, source_target_pairs={{2,0},{4,2},{6,4},{8,6},{10,8},{12,10},{14,12},{3,1},{5,3},{7,5},{... | collective-permute-start | bytes 196616 | tf_op jit(solution)/shard_map/ppermute | solution.py:17
  12.0 3.4 %collective-permute-start.2 = (bf16[34,1,128]{2,1,0:T(2,128)(2,1)S(1)}, bf16[34,1,128]{2,1,0:T(2,128)(2,1)S(1)}, u32[]{:S(2)}, u32[]{:S(2)}) collective-permute-start(bf16[34,1,128]{2,1,0:T(2,128)(2,1)S(1)} %get-tuple-element.13), channel_id=1, source_target_pairs={{0,1},{2,3},{4,5},{6,7},{8,9},{10,11},{12,13},{14,15},{16,17},{18,... | collective-permute-start | bytes 26120 | tf_op jit(solution)/shard_map/ppermute | solution.py:16
  13.3 3.1 %collective-permute-start.3 = (bf16[34,1,128]{2,1,0:T(2,128)(2,1)S(1)}, bf16[34,1,128]{2,1,0:T(2,128)(2,1)S(1)}, u32[]{:S(2)}, u32[]{:S(2)}) collective-permute-start(bf16[34,1,128]{2,1,0:T(2,128)(2,1)S(1)} %get-tuple-element.14), channel_id=1, source_target_pairs={{1,0},{3,2},{5,4},{7,6},{9,8},{11,10},{13,12},{15,14},{17,16},{19,... | collective-permute-start | bytes 26120 | tf_op jit(solution)/shard_map/ppermute | solution.py:17
  30.7 1.8 %copy-start.1 = (f32[128]{0:T(128)S(1)}, f32[128]{0:T(128)}, u32[]{:S(2)}) copy-start(f32[128]{0:T(128)} %param.9) | copy-start | bytes 1540
  32.6 14.1 %copy-start = (bf16[3,3,128,128]{3,2,1,0:T(8,128)(2,1)S(1)}, bf16[3,3,128,128]{3,2,1,0:T(8,128)(2,1)}, u32[]{:S(2)}) copy-start(bf16[3,3,128,128]{3,2,1,0:T(8,128)(2,1)} %param.10) | copy-start | bytes 884740
  33.3 6.2 %collective-permute-start.4 = (bf16[1,256,128]{2,1,0:T(8,128)(2,1)S(1)}, bf16[1,256,128]{2,1,0:T(8,128)(2,1)S(1)}, u32[]{:S(2)}, u32[]{:S(2)}) collective-permute-start(bf16[1,256,128]{2,1,0:T(8,128)(2,1)S(1)} %get-tuple-element.15), channel_id=1, source_target_pairs={{0,2},{2,4},{4,6},{6,8},{8,10},{10,12},{12,14},{1,3},{3,5},{5,7},{... | collective-permute-start | bytes 196616 | tf_op jit(solution)/shard_map/ppermute | solution.py:16
  37.7 6.2 %collective-permute-start.5 = (bf16[1,256,128]{2,1,0:T(8,128)(2,1)S(1)}, bf16[1,256,128]{2,1,0:T(8,128)(2,1)S(1)}, u32[]{:S(2)}, u32[]{:S(2)}) collective-permute-start(bf16[1,256,128]{2,1,0:T(8,128)(2,1)S(1)} %get-tuple-element.16), channel_id=1, source_target_pairs={{2,0},{4,2},{6,4},{8,6},{10,8},{12,10},{14,12},{3,1},{5,3},{7,5},{... | collective-permute-start | bytes 196616 | tf_op jit(solution)/shard_map/ppermute | solution.py:17
  43.9 2.8 %collective-permute-start.6 = (bf16[34,1,128]{2,1,0:T(2,128)(2,1)S(1)}, bf16[34,1,128]{2,1,0:T(2,128)(2,1)S(1)}, u32[]{:S(2)}, u32[]{:S(2)}) collective-permute-start(bf16[34,1,128]{2,1,0:T(2,128)(2,1)S(1)} %get-tuple-element.11), channel_id=1, source_target_pairs={{0,1},{2,3},{4,5},{6,7},{8,9},{10,11},{12,13},{14,15},{16,17},{18,... | collective-permute-start | bytes 26120 | tf_op jit(solution)/shard_map/ppermute | solution.py:16
  45.2 3.1 %collective-permute-start.7 = (bf16[34,1,128]{2,1,0:T(2,128)(2,1)S(1)}, bf16[34,1,128]{2,1,0:T(2,128)(2,1)S(1)}, u32[]{:S(2)}, u32[]{:S(2)}) collective-permute-start(bf16[34,1,128]{2,1,0:T(2,128)(2,1)S(1)} %get-tuple-element.12), channel_id=1, source_target_pairs={{1,0},{3,2},{5,4},{7,6},{9,8},{11,10},{13,12},{15,14},{17,16},{19,... | collective-permute-start | bytes 26120 | tf_op jit(solution)/shard_map/ppermute | solution.py:17
  68.3 1.8 %copy-start.2 = (f32[128]{0:T(128)S(1)}, f32[128]{0:T(128)}, u32[]{:S(2)}) copy-start(f32[128]{0:T(128)} %param.11) | copy-start | bytes 1540
where the time goes:
time: 72.5 us; the launch traced here: 72.1 us
  other arithmetic  18.1 us (25%)
  starting transfers between devices  17.2 us (24%)
  local copies, waits for them, and re-layouts  16.6 us (23%)
  matrix products  10.8 us (15%)
  waiting for transfers between devices  9.24 us (13%)
    concatenate x2, other arithmetic, conv_valid(): jnp.concatenate([padded[:, 0:cols], padded[:, 1:cols + 1], padded[:, 2:co...  14.6 us
    slice x2, local copies, waits for them, and re-layouts, conv_valid(): block = wide[offset:offset + rows].reshape(rows * cols, 3 * chans)  12.5 us
    ppermute x4, starting transfers between devices, with_halo(): before = lax.ppermute(last, axis, up)  11.8 us
    dot_general x6, matrix products, conv_valid(): jnp.dot(block, kernel[offset].reshape(3 * chans, kernel.shape[3]), prefer...  10.8 us
    ppermute x4, waiting for transfers between devices, with_halo(): after = lax.ppermute(leading, axis, down)  8.65 us
    ppermute x4, starting transfers between devices, with_halo(): after = lax.ppermute(leading, axis, down)  5.35 us
    convert_element_type x1, other arithmetic, shards(): return (jnp.maximum(result, 0.0) * pixel_mask).astype(jnp.bfloat16)  2.03 us
    unnamed x8, local copies, waits for them, and re-layouts  1.98 us
  transfers between devices with their start and end apart: 8, of which 5 were waited for; matrix products, arithmetic and copies ran while one was open for 5% of the time, Pallas kernels for 0%

commit v1 on v0

v1 whole, which is shorter than its diff:
```python
import functools

import jax
import jax.numpy as jnp
from jax import lax
from jax.experimental import pallas as pl
from jax.experimental.pallas import tpu as pltpu
from jax.sharding import PartitionSpec as P

MB = 32
EDGE = 8
AROUND = [(dr, dc) for dr in (-1, 0, 1) for dc in (-1, 0, 1) if (dr, dc) != (0, 0)]


def largest_divisor(count, most):
    return max(d for d in range(1, most + 1) if count % d == 0)


def kernel(
    grid,
    img,
    tis,
    k1,
    b1,
    k2,
    b2,
    out,
    x,
    h,
    o,
    w1,
    w2,
    tiles,
    mask,
    load_sem,
    w_sem,
    out_sem,
    send_sem,
    recv_sem,
):
    n_rows, n_cols = grid
    rows, cols, chans = img.shape
    t_rows, t_cols = tis.shape[0], tis.shape[1]
    span = cols + 2 * EDGE
    r, c = lax.axis_index("rows"), lax.axis_index("cols")

    def has(dr, dc):
        ok = jnp.bool_(True)
        if dr:
            ok = ok & (r + dr >= 0) & (r + dr < n_rows)
        if dc:
            ok = ok & (c + dc >= 0) & (c + dc < n_cols)
        return ok

    def whom(dr, dc):
        where = {}
        if dr:
            where["rows"] = r + dr
        if dc:
            where["cols"] = c + dc
        return where

    to_rows = {-1: (0, 2), 0: (2, rows), 1: (rows + 2, 2)}
    to_cols = {-1: (cols + EDGE, EDGE), 0: (0, cols), 1: (cols, EDGE)}
    from_rows = {-1: (rows - 2, 2), 0: (0, rows), 1: (0, 2)}
    from_cols = {-1: (cols - EDGE, EDGE), 0: (0, cols), 1: (0, EDGE)}

    def place(dr, dc):
        return x.at[pl.ds(*to_rows[dr]), pl.ds(*to_cols[dc]), :]

    def copies(n, dr, dc):
        pixels = pltpu.make_async_remote_copy(
            src_ref=img.at[pl.ds(*from_rows[dr]), pl.ds(*from_cols[dc]), :],
            dst_ref=place(dr, dc),
            send_sem=send_sem.at[2 * n],
            recv_sem=recv_sem.at[2 * n],
            device_id=whom(-dr, -dc),
            device_id_type=pl.DeviceIdType.MESH,
        )
        tissue = pltpu.make_async_remote_copy(
            src_ref=tis,
            dst_ref=tiles.at[n],
            send_sem=send_sem.at[2 * n + 1],
            recv_sem=recv_sem.at[2 * n + 1],
            device_id=whom(-dr, -dc),
            device_id_type=pl.DeviceIdType.MESH,
        )
        return pixels, tissue

    barrier = pltpu.get_barrier_semaphore()
    for dr, dc in AROUND:

        @pl.when(has(dr, dc))
        def _():
            pl.semaphore_signal(
                barrier,
                inc=1,
                device_id=whom(dr, dc),
                device_id_type=pl.DeviceIdType.MESH,
            )

    load = pltpu.make_async_copy(img, place(0, 0), load_sem)
    load.start()
    weights = []
    for n, (k, w) in enumerate(((k1, w1), (k2, w2))):
        for half in (0, 1):
            weights.append(
                pltpu.make_async_copy(
                    k,
                    w.at[pl.ds(half, 3), :, :, pl.ds(half * chans, chans)],
                    w_sem.at[2 * n + half],
                )
            )
            weights[-1].start()
    for n, (dr, dc) in enumerate(AROUND):

        @pl.when(jnp.logical_not(has(dr, dc)))
        def _():
            at = (pl.ds(*to_rows[dr]), pl.ds(*to_cols[dc]))
            x[at] = jnp.zeros((to_rows[dr][1], to_cols[dc][1], chans), x.dtype)
            tiles[n] = jnp.zeros(tiles.shape[1:], tiles.dtype)

    present = [jnp.where(has(dr, dc), 1, 0) for dr, dc in AROUND]
    pl.semaphore_wait(barrier, sum(present))

    order = sorted(enumerate(AROUND), key=lambda p: (p[1][0] != 0, p[1][1] != 0))
    for n, (dr, dc) in order:

        @pl.when(has(-dr, -dc))
        def _():
            for copy in copies(n, dr, dc):
                copy.start()

    for w in (w1, w2):
        for s in range(3):
            w[3, s, :, :chans] = jnp.zeros((chans, chans), w.dtype)
            w[0, s, :, chans:] = jnp.zeros((chans, chans), w.dtype)

    def receive(which):
        for n, (dr, dc) in enumerate(AROUND):
            if (dr != 0) == which:

                @pl.when(has(dr, dc))
                def _():
                    for copy in copies(n, dr, dc):
                        copy.wait_recv()

    def put_mask(at, middle, right, left):
        for b in range(t_cols):
            mask[at, b * MB : (b + 1) * MB, :] = jnp.broadcast_to(
                middle[b : b + 1], (MB, chans)
            )
        mask[at, cols : cols + EDGE, :] = jnp.broadcast_to(right[0:1], (EDGE, chans))
        mask[at, cols + EDGE :, :] = jnp.broadcast_to(
            left[t_cols - 1 : t_cols], (EDGE, chans)
        )

    index = {d: n for n, d in enumerate(AROUND)}

    def conv(src, first, group, w, bias, emit):
        lhs = jnp.concatenate(
            [
                jnp.concatenate([src[first + 2 * g + k] for k in range(4)], axis=1)
                for g in range(group)
            ],
            axis=0,
        )
        parts = []
        for s in range(3):
            weight = w[:, s].reshape(4 * chans, 2 * chans)
            parts.append(jnp.dot(lhs, weight, preferred_element_type=jnp.float32))
        b = bias[...]
        for g in range(group):
            y = [p[g * span : (g + 1) * span] for p in parts]
            total = y[1] + pltpu.roll(y[0], 1, 0) + pltpu.roll(y[2], span - 1, 0)
            for half in (0, 1):
                value = total[:, half * chans : (half + 1) * chans] + b
                emit(first + 2 * g + half, jnp.maximum(value, 0.0))

    def hide(row, value):
        h[row] = (value * mask[(row + MB - 1) // MB]).astype(h.dtype)

    def show(row, value):
        o[row] = (value[:cols] * mask[row // MB + 1, :cols]).astype(o.dtype)

    receive(False)
    for t in range(t_rows):
        put_mask(1 + t, tis[t], tiles[index[0, 1], t], tiles[index[0, -1], t])
    load.wait()
    for copy in weights:
        copy.wait()

    inner1 = rows // 2 - 1
    g1 = largest_divisor(inner1, 3)

    def first_body(i, _):
        conv(x, 2 + 2 * g1 * i, g1, w1, b1, hide)
        return 0

    lax.fori_loop(0, inner1 // g1, first_body, 0)

    inner2 = rows // 2 - 2
    g2 = largest_divisor(inner2, 3)
    turns = inner2 // g2

    def put(i, start, length):
        at = pl.ds(start, length)
        return pltpu.make_async_copy(o.at[at], out.at[at], out_sem.at[i])

    def second_body(i, _):
        start = 2 + 2 * g2 * i
        conv(h, start, g2, w2, b2, show)
        put(i, start, 2 * g2).start()
        return 0

    lax.fori_loop(0, turns, second_body, 0)

    receive(True)
    for dr, at, t in ((-1, 0, t_rows - 1), (1, t_rows + 1, 0)):
        put_mask(
            at,
            tiles[index[dr, 0], t],
            tiles[index[dr, 1], t],
            tiles[index[dr, -1], t],
        )
    for row in (0, rows):
        conv(x, row, 1, w1, b1, hide)
    for n, row in enumerate((0, rows - 2)):
        conv(h, row, 1, w2, b2, show)
        put(turns + n, row, 2).start()

    for i in range(turns):
        put(i, 2 + 2 * g2 * i, 2 * g2).wait()
    for n, row in enumerate((0, rows - 2)):
        put(turns + n, row, 2).wait()
    for n, (dr, dc) in enumerate(AROUND):

        @pl.when(has(-dr, -dc))
        def _():
            for copy in copies(n, dr, dc):
                copy.wait_send()


def shards(image, tissue, first_kernel, first_bias, second_kernel, second_bias):
    rows, cols, chans = image.shape
    t_rows, t_cols = tissue.shape
    grid = (lax.axis_size("rows"), lax.axis_size("cols"))
    tis = jnp.broadcast_to(
        tissue.astype(jnp.float32)[:, :, None], (t_rows, t_cols, chans)
    )
    span = cols + 2 * EDGE
    vmem = pl.BlockSpec(memory_space=pltpu.VMEM)
    anywhere = pl.BlockSpec(memory_space=pl.ANY)
    return pl.pallas_call(
        functools.partial(kernel, grid),
        out_shape=jax.ShapeDtypeStruct((rows, cols, chans), jnp.bfloat16),
        in_specs=[anywhere, vmem, anywhere, vmem, anywhere, vmem],
        out_specs=anywhere,
        scratch_shapes=[
            pltpu.VMEM((rows + 4, span, chans), jnp.bfloat16),
            pltpu.VMEM((rows + 2, span, chans), jnp.bfloat16),
            pltpu.VMEM((rows, cols, chans), jnp.bfloat16),
            pltpu.VMEM((4, 3, chans, 2 * chans), jnp.bfloat16),
            pltpu.VMEM((4, 3, chans, 2 * chans), jnp.bfloat16),
            pltpu.VMEM((len(AROUND), t_rows, t_cols, chans), jnp.float32),
            pltpu.VMEM((t_rows + 2, span, chans), jnp.float32),
            pltpu.SemaphoreType.DMA,
            pltpu.SemaphoreType.DMA((4,)),
            pltpu.SemaphoreType.DMA((rows // 2,)),
            pltpu.SemaphoreType.DMA((2 * len(AROUND),)),
            pltpu.SemaphoreType.DMA((2 * len(AROUND),)),
        ],
        compiler_params=pltpu.CompilerParams(collective_id=0, has_side_effects=True),
    )(
        image,
        tis,
        first_kernel,
        first_bias.reshape(1, -1),
        second_kernel,
        second_bias.reshape(1, -1),
    )


def solution(mesh):
    in_specs = (
        P(("slides", "rows"), "cols", None),
        P(("slides", "rows"), "cols"),
        P(),
        P(),
        P(),
        P(),
    )
    out_specs = P(("slides", "rows"), "cols", None)
    return jax.shard_map(shards, mesh=mesh, in_specs=in_specs, out_specs=out_specs, check_vma=False)
```

time: 72.5 us -> 20.1 us (0.28)
  other arithmetic: 18.1 us -> 0.66 us
  starting transfers between devices: 17.2 us -> 0 us
  Pallas kernels: 0 us -> 15.5 us
  local copies, waits for them, and re-layouts: 16.6 us -> 3.8 us
  matrix products: 10.8 us -> 0 us
  waiting for transfers between devices: 9.24 us -> 0 us
    ppermute x8 -> x0, starting transfers between devices: 17.2 us -> none  [the longest x4 11.8 us: with_halo(): before = lax.ppermute(last, axis, up)]
    pallas_call x0 -> x1, Pallas kernels: none -> 15.5 us  [shards(): pl.pallas_call(functools.partial(kernel, grid), out_shape=jax.ShapeDtypeS...]
    concatenate x2 -> x0, other arithmetic: 14.6 us -> none  [conv_valid(): jnp.concatenate([padded[:, 0:cols], padded[:, 1:cols + 1], padded[:, 2:co...]
    slice x7 -> x0, local copies, waits for them, and re-layouts: 14.5 us -> none  [the longest x2 12.5 us: conv_valid(): block = wide[offset:offset + rows].reshape(rows * cols, 3 * chans)]
    dot_general x6 -> x0, matrix products: 10.8 us -> none  [conv_valid(): jnp.dot(block, kernel[offset].reshape(3 * chans, kernel.shape[3]), prefer...]
    ppermute x8 -> x0, waiting for transfers between devices: 9.24 us -> none  [the longest x4 8.65 us: with_halo(): after = lax.ppermute(leading, axis, down)]
    convert_element_type x3 -> x0, other arithmetic: 3.43 us -> none  [the longest x1 2.03 us: shards(): return (jnp.maximum(result, 0.0) * pixel_mask).astype(jnp.bfloat16)]
    unnamed x8 -> x1, local copies, waits for them, and re-layouts: 1.98 us -> 3.14 us
  transfers between devices with their start and end apart: 8 -> 0, of which waited for: 5 -> 0; matrix products, arithmetic and copies ran while one was open for 5% -> 0% of each run, Pallas kernels for 0% -> 0%
where the time goes in v1:
time: 20.1 us; the launch traced here: 19.9 us
  Pallas kernels  15.5 us (77%)
  local copies, waits for them, and re-layouts  3.8 us (19%)
  other arithmetic  0.66 us (3%)
    pallas_call x1, Pallas kernels, shards(): pl.pallas_call(functools.partial(kernel, grid), out_shape=jax.ShapeDtypeS...  15.5 us
    unnamed x1, local copies, waits for them, and re-layouts  3.14 us
    broadcast_in_dim x1, local copies, waits for them, and re-layouts, shards(): jnp.broadcast_to(tissue.astype(jnp.float32)[:, :, None], (t_rows, t_cols,...  0.66 us
    broadcast_in_dim x1, other arithmetic, shards(): jnp.broadcast_to(tissue.astype(jnp.float32)[:, :, None], (t_rows, t_cols,...  0.66 us

profile of v1, /device:TPU:0, one launch (start us, length us, event | category | flops | bytes accessed | tf_op | source)
XLA Modules:
  0.0 19.9 jit_solution(6285827924131089582)
XLA Ops:
  0.0 0.7 %convert_bitcast_fusion = f32[8]{0:T(128)S(1)} fusion(s32[1,8]{1,0:T(1,128)} %param.7), kind=kLoop, calls=%fused_computation | loop fusion | flops 8 | bytes 64 | tf_op jit(solution)/shard_map/broadcast_in_dim | solution.py:248
  0.7 0.7 %broadcast_in_dim.9.tis = f32[1,8,128]{2,1,0:T(8,128)} broadcast(f32[8]{0:T(128)S(1)} %convert_bitcast_fusion), dimensions={1} | broadcast | bytes 4128 | tf_op jit(solution)/shard_map/broadcast_in_dim | solution.py:248
  1.3 15.5 %shard_map.64 = bf16[32,256,128]{2,1,0:T(8,128)(2,1)} custom-call(bf16[32,256,128]{2,1,0:T(8,128)(2,1)} %img.1, f32[1,8,128]{2,1,0:T(8,128)} %broadcast_in_dim.9.tis, bf16[3,3,128,128]{3,2,1,0:T(8,128)(2,1)} %k1.1, f32[1,128]{1,0:T(1,128)} %bitcast.4, bf16[3,3,128,128]{3,2,1,0:T(8,128)(2,1)} %k2.1, f32[1,128]{1,0:T(1,128)} %bitcast.5), custom_call_target="tpu_custom_call" | custom-call | tf_op jit(solution)/shard_map/pallas_call | solution.py:254
  16.8 3.1 %copy.8 = bf16[32,256,128]{2,1,0:T(8,128)(2,1)} copy(bf16[32,256,128]{2,1,0:T(8,128)(2,1)} %shard_map.64) | data formatting | bytes 4194304

commit v2 on v1

v2 whole, which is shorter than its diff:
```python
import functools

import jax
import jax.numpy as jnp
from jax import lax
from jax.experimental import pallas as pl
from jax.experimental.pallas import tpu as pltpu
from jax.sharding import PartitionSpec as P

MB = 32
VMEM_INNER = 32 * 2**20
VMEM_OUTER = 16 * 2**20
EDGE = 8
AROUND = [(dr, dc) for dr in (-1, 0, 1) for dc in (-1, 0, 1) if (dr, dc) != (0, 0)]


def largest_divisor(count, most):
    return max(d for d in range(1, most + 1) if count % d == 0)


def conv(src, firsts, w, bias, emit):
    span, chans = src.shape[1:]
    lhs = jnp.concatenate(
        [jnp.concatenate([src[f + k] for k in range(4)], axis=1) for f in firsts],
        axis=0,
    )
    parts = []
    for s in range(3):
        weight = w[:, s].reshape(4 * chans, 2 * chans)
        parts.append(jnp.dot(lhs, weight, preferred_element_type=jnp.float32))
    b = bias[...]
    for g, first in enumerate(firsts):
        y = [p[g * span : (g + 1) * span] for p in parts]
        total = y[1] + pltpu.roll(y[0], 1, 0) + pltpu.roll(y[2], span - 1, 0)
        for half in (0, 1):
            value = total[:, half * chans : (half + 1) * chans] + b
            emit(first + half, jnp.maximum(value, 0.0))


def inner_kernel(
    grid,
    img,
    tis_in,
    k1,
    b1_in,
    k2,
    b2_in,
    h,
    o,
    w2,
    mask,
    b2,
    x,
    w1,
    b1,
    tis,
    tiles,
    load_sem,
    w_sem,
    small_sem,
    send_sem,
    recv_sem,
):
    n_rows, n_cols = grid
    rows, cols, chans = img.shape
    t_rows, t_cols = tis.shape
    r, c = lax.axis_index("rows"), lax.axis_index("cols")

    def has(dr, dc):
        ok = jnp.bool_(True)
        if dr:
            ok = ok & (r + dr >= 0) & (r + dr < n_rows)
        if dc:
            ok = ok & (c + dc >= 0) & (c + dc < n_cols)
        return ok

    def whom(dr, dc):
        where = {}
        if dr:
            where["rows"] = r + dr
        if dc:
            where["cols"] = c + dc
        return where

    to_rows = {-1: (0, 2), 0: (2, rows), 1: (rows + 2, 2)}
    to_cols = {-1: (cols + EDGE, EDGE), 0: (0, cols), 1: (cols, EDGE)}
    from_rows = {-1: (rows, 2), 0: (2, rows), 1: (2, 2)}
    from_cols = {-1: (cols - EDGE, EDGE), 0: (0, cols), 1: (0, EDGE)}

    def pixels(n, dr, dc):
        return pltpu.make_async_remote_copy(
            src_ref=x.at[pl.ds(*from_rows[dr]), pl.ds(*from_cols[dc]), :],
            dst_ref=x.at[pl.ds(*to_rows[dr]), pl.ds(*to_cols[dc]), :],
            send_sem=send_sem.at[2 * n],
            recv_sem=recv_sem.at[2 * n],
            device_id=whom(-dr, -dc),
            device_id_type=pl.DeviceIdType.MESH,
        )

    def tissue(n, dr, dc):
        return pltpu.make_async_remote_copy(
            src_ref=tis,
            dst_ref=tiles.at[n],
            send_sem=send_sem.at[2 * n + 1],
            recv_sem=recv_sem.at[2 * n + 1],
            device_id=whom(-dr, -dc),
            device_id_type=pl.DeviceIdType.MESH,
        )

    barrier = pltpu.get_barrier_semaphore()
    for dr, dc in AROUND:

        @pl.when(has(dr, dc))
        def _():
            pl.semaphore_signal(
                barrier,
                inc=1,
                device_id=whom(dr, dc),
                device_id_type=pl.DeviceIdType.MESH,
            )

    loads = []
    for n, (start, length) in enumerate(((0, 2), (rows - 2, 2), (2, rows - 4))):
        loads.append(
            pltpu.make_async_copy(
                img.at[pl.ds(start, length)],
                x.at[pl.ds(2 + start, length), pl.ds(0, cols), :],
                load_sem.at[n],
            )
        )
        loads[-1].start()
    smalls = []
    for n, (src, dst) in enumerate(((tis_in, tis), (b1_in, b1), (b2_in, b2))):
        smalls.append(pltpu.make_async_copy(src, dst, small_sem.at[n]))
        smalls[-1].start()
    weights = []
    for n, (k, w) in enumerate(((k1, w1), (k2, w2))):
        for half in (0, 1):
            weights.append(
                pltpu.make_async_copy(
                    k,
                    w.at[pl.ds(half, 3), :, :, pl.ds(half * chans, chans)],
                    w_sem.at[2 * n + half],
                )
            )
            weights[-1].start()
    for n, (dr, dc) in enumerate(AROUND):

        @pl.when(jnp.logical_not(has(dr, dc)))
        def _():
            at = (pl.ds(*to_rows[dr]), pl.ds(*to_cols[dc]))
            x[at] = jnp.zeros((to_rows[dr][1], to_cols[dc][1], chans), x.dtype)
            tiles[n] = jnp.zeros(tiles.shape[1:], tiles.dtype)

    for copy in loads[:2]:
        copy.wait()
    smalls[0].wait()
    present = [jnp.where(has(dr, dc), 1, 0) for dr, dc in AROUND]
    pl.semaphore_wait(barrier, sum(present))

    def send(which, make):
        for n, (dr, dc) in enumerate(AROUND):
            if (dr != 0) == which:

                @pl.when(has(-dr, -dc))
                def _():
                    make(n, dr, dc).start()

    send(True, pixels)
    send(False, tissue)
    loads[2].wait()
    send(False, pixels)
    send(True, tissue)

    for w in (w1, w2):
        for s in range(3):
            w[3, s, :, :chans] = jnp.zeros((chans, chans), w.dtype)
            w[0, s, :, chans:] = jnp.zeros((chans, chans), w.dtype)

    def receive(which):
        for n, (dr, dc) in enumerate(AROUND):
            if (dr != 0) == which:

                @pl.when(has(dr, dc))
                def _():
                    tissue(n, dr, dc).wait_recv()
                    pixels(n, dr, dc).wait_recv()

    def put_mask(at, middle, right, left):
        def wide(values, b, length):
            value = values[:, b : b + 1].astype(jnp.float32)
            return jnp.broadcast_to(value, (length, chans))

        for b in range(t_cols):
            mask[at, b * MB : (b + 1) * MB, :] = wide(middle, b, MB)
        mask[at, cols : cols + EDGE, :] = wide(right, 0, EDGE)
        mask[at, cols + EDGE :, :] = wide(left, t_cols - 1, EDGE)

    index = {d: n for n, d in enumerate(AROUND)}

    def hide(row, value):
        h[row] = (value * mask[(row + MB - 1) // MB]).astype(h.dtype)

    def show(row, value):
        o[row] = (value[:cols] * mask[row // MB + 1, :cols]).astype(o.dtype)

    for copy in smalls[1:]:
        copy.wait()
    for copy in weights:
        copy.wait()
    receive(False)
    for t in range(t_rows):
        at = pl.ds(t, 1)
        put_mask(1 + t, tis[at], tiles[index[0, 1], at], tiles[index[0, -1], at])

    inner1 = rows // 2 - 1
    g1 = largest_divisor(inner1, 3)

    def first_body(i, _):
        conv(x, [2 + 2 * (g1 * i + g) for g in range(g1)], w1, b1, hide)
        return 0

    lax.fori_loop(0, inner1 // g1, first_body, 0)

    inner2 = rows // 2 - 2
    g2 = largest_divisor(inner2, 3)

    def second_body(i, _):
        conv(h, [2 + 2 * (g2 * i + g) for g in range(g2)], w2, b2, show)
        return 0

    lax.fori_loop(0, inner2 // g2, second_body, 0)

    receive(True)
    for dr, at, t in ((-1, 0, t_rows - 1), (1, t_rows + 1, 0)):
        put_mask(at, *[tiles[index[dr, dc], pl.ds(t, 1)] for dc in (0, 1, -1)])
    conv(x, [0, rows], w1, b1, hide)
    for n, (dr, dc) in enumerate(AROUND):

        @pl.when(has(-dr, -dc))
        def _():
            pixels(n, dr, dc).wait_send()
            tissue(n, dr, dc).wait_send()


def outer_kernel(h, o, w2, mask, b2, out, e, sem):
    rows, cols, _ = o.shape
    pieces = largest_divisor(rows - 4, 4)
    length = (rows - 4) // pieces
    copies = []
    for n in range(pieces):
        at = pl.ds(2 + n * length, length)
        copies.append(pltpu.make_async_copy(o.at[at], out.at[at], sem.at[n]))
        copies[-1].start()

    def show(row, value):
        at = row if row < 2 else row - rows + 4
        e[at] = (value[:cols] * mask[row // MB + 1, :cols]).astype(e.dtype)

    conv(h, [0, rows - 2], w2, b2, show)
    for n, row in enumerate((0, rows - 2)):
        copies.append(
            pltpu.make_async_copy(
                e.at[pl.ds(2 * n, 2)], out.at[pl.ds(row, 2)], sem.at[pieces + n]
            )
        )
        copies[-1].start()
    for copy in copies:
        copy.wait()


def shards(image, tissue, first_kernel, first_bias, second_kernel, second_bias):
    rows, cols, chans = image.shape
    t_rows, t_cols = tissue.shape
    grid = (lax.axis_size("rows"), lax.axis_size("cols"))
    span = cols + 2 * EDGE
    vmem = pl.BlockSpec(memory_space=pltpu.VMEM)
    anywhere = pl.BlockSpec(memory_space=pltpu.HBM)
    held = pl.pallas_call(
        functools.partial(inner_kernel, grid),
        out_shape=[
            pltpu.VMEM((rows + 2, span, chans), jnp.bfloat16),
            pltpu.VMEM((rows, cols, chans), jnp.bfloat16),
            pltpu.VMEM((4, 3, chans, 2 * chans), jnp.bfloat16),
            pltpu.VMEM((t_rows + 2, span, chans), jnp.float32),
            pltpu.VMEM((1, chans), jnp.float32),
        ],
        in_specs=[anywhere] * 6,
        out_specs=[vmem] * 5,
        scratch_shapes=[
            pltpu.VMEM((rows + 4, span, chans), jnp.bfloat16),
            pltpu.VMEM((4, 3, chans, 2 * chans), jnp.bfloat16),
            pltpu.VMEM((1, chans), jnp.float32),
            pltpu.VMEM((t_rows, t_cols), jnp.int32),
            pltpu.VMEM((len(AROUND), t_rows, t_cols), jnp.int32),
            pltpu.SemaphoreType.DMA((3,)),
            pltpu.SemaphoreType.DMA((4,)),
            pltpu.SemaphoreType.DMA((3,)),
            pltpu.SemaphoreType.DMA((2 * len(AROUND),)),
            pltpu.SemaphoreType.DMA((2 * len(AROUND),)),
        ],
        compiler_params=pltpu.CompilerParams(
            collective_id=0, has_side_effects=True, vmem_limit_bytes=VMEM_INNER
        ),
    )(
        *[
            pltpu.with_memory_space_constraint(value, pltpu.HBM)
            for value in (
                image,
                tissue,
                first_kernel,
                first_bias.reshape(1, -1),
                second_kernel,
                second_bias.reshape(1, -1),
            )
        ]
    )
    return pl.pallas_call(
        outer_kernel,
        out_shape=jax.ShapeDtypeStruct((rows, cols, chans), jnp.bfloat16),
        in_specs=[vmem] * 5,
        out_specs=anywhere,
        scratch_shapes=[
            pltpu.VMEM((4, cols, chans), jnp.bfloat16),
            pltpu.SemaphoreType.DMA((8,)),
        ],
        compiler_params=pltpu.CompilerParams(vmem_limit_bytes=VMEM_OUTER),
    )(*held)


def solution(mesh):
    in_specs = (
        P(("slides", "rows"), "cols", None),
        P(("slides", "rows"), "cols"),
        P(),
        P(),
        P(),
        P(),
    )
    out_specs = P(("slides", "rows"), "cols", None)
    return jax.shard_map(shards, mesh=mesh, in_specs=in_specs, out_specs=out_specs, check_vma=False)
```

time: 20.1 us -> 15 us (0.75)
  local copies, waits for them, and re-layouts: 3.8 us -> 0 us
  Pallas kernels: 15.5 us -> 14.8 us
  other arithmetic: 0.66 us -> 0 us
    unnamed x1 -> x0, local copies, waits for them, and re-layouts: 3.14 us -> none
    broadcast_in_dim x1 -> x0, local copies, waits for them, and re-layouts: 0.66 us -> none  [shards(): jnp.broadcast_to(tissue.astype(jnp.float32)[:, :, None], (t_rows, t_cols,...]
    broadcast_in_dim x1 -> x0, other arithmetic: 0.66 us -> none  [shards(): jnp.broadcast_to(tissue.astype(jnp.float32)[:, :, None], (t_rows, t_cols,...]
    pallas_call x1 -> x2, Pallas kernels: 15.5 us -> 14.8 us  [the longest x1 13.5 us: shards(): pl.pallas_call(functools.partial(inner_kernel, grid), out_shape=[pltpu.VM...]
where the time goes in v2:
time: 15 us; the launch traced here: 14.8 us
  Pallas kernels  14.8 us (99%)
    pallas_call x1, Pallas kernels, shards(): pl.pallas_call(functools.partial(inner_kernel, grid), out_shape=[pltpu.VM...  13.5 us
    pallas_call x1, Pallas kernels, shards(): pl.pallas_call(outer_kernel, out_shape=jax.ShapeDtypeStruct((rows, cols,...  1.39 us

profile of v2, /device:TPU:0, one launch (start us, length us, event | category | flops | bytes accessed | tf_op | source)
XLA Modules:
  0.0 14.8 jit_solution(13382740312023669266)
XLA Ops:
  0.0 13.5 %shard_map.64 = (bf16[34,272,128]{2,1,0:T(8,128)(2,1)S(1)}, bf16[32,256,128]{2,1,0:T(8,128)(2,1)S(1)}, bf16[4,3,128,256]{3,2,1,0:T(8,128)(2,1)S(1)}, f32[3,272,128]{2,1,0:T(8,128)S(1)}, f32[1,128]{1,0:T(1,128)S(1)}) custom-call(bf16[32,256,128]{2,1,0:T(8,128)(2,1)} %img.1, s32[1,8]{1,0:T(1,128)} %tis_in.1, bf16[3,3,128,128]{3,2,1,0:T(8,128)(2,1)} %k1.1, ...), custom_call_target="tpu_custom_call" | custom-call | tf_op jit(solution)/shard_map/pallas_call | solution.py:279
  13.5 1.4 %shard_map.65 = bf16[32,256,128]{2,1,0:T(8,128)(2,1)} custom-call(bf16[34,272,128]{2,1,0:T(8,128)(2,1)S(1)} %get-tuple-element.10.h, bf16[32,256,128]{2,1,0:T(8,128)(2,1)S(1)} %get-tuple-element.11.o, bf16[4,3,128,256]{3,2,1,0:T(8,128)(2,1)S(1)} %get-tuple-element.12.w2, f32[3,272,128]{2,1,0:T(8,128)S(1)} %get-tuple-element.13.mask, ...), custom_call_target="tpu_custom_call" | custom-call | tf_op jit(solution)/shard_map/pallas_call | solution.py:318

commit v3 on v2

--- a/solution.py
+++ b/solution.py
@@ -18,10 +18,17 @@
     return max(d for d in range(1, most + 1) if count % d == 0)
 
 
-def conv(src, firsts, w, bias, emit):
-    span, chans = src.shape[1:]
+def conv(src, firsts, w, bias, emit, pieces=None):
+    pieces = pieces or ((0, src.shape[1]),)
+    span, chans = sum(length for _, length in pieces), src.shape[2]
     lhs = jnp.concatenate(
-        [jnp.concatenate([src[f + k] for k in range(4)], axis=1) for f in firsts],
+        [
+            jnp.concatenate(
+                [src[f + k, start : start + length] for k in range(4)], axis=1
+            )
+            for f in firsts
+            for start, length in pieces
+        ],
         axis=0,
     )
     parts = []
@@ -152,6 +159,11 @@
             x[at] = jnp.zeros((to_rows[dr][1], to_cols[dc][1], chans), x.dtype)
             tiles[n] = jnp.zeros(tiles.shape[1:], tiles.dtype)
 
+    for w in (w1, w2):
+        for s in range(3):
+            w[3, s, :, :chans] = jnp.zeros((chans, chans), w.dtype)
+            w[0, s, :, chans:] = jnp.zeros((chans, chans), w.dtype)
+
     for copy in loads[:2]:
         copy.wait()
     smalls[0].wait()
@@ -172,11 +184,6 @@
     send(False, pixels)
     send(True, tissue)
 
-    for w in (w1, w2):
-        for s in range(3):
-            w[3, s, :, :chans] = jnp.zeros((chans, chans), w.dtype)
-            w[0, s, :, chans:] = jnp.zeros((chans, chans), w.dtype)
-
     def receive(which):
         for n, (dr, dc) in enumerate(AROUND):
             if (dr != 0) == which:
@@ -186,13 +193,15 @@
                     tissue(n, dr, dc).wait_recv()
                     pixels(n, dr, dc).wait_recv()
 
-    def put_mask(at, middle, right, left):
-        def wide(values, b, length):
-            value = values[:, b : b + 1].astype(jnp.float32)
-            return jnp.broadcast_to(value, (length, chans))
-
+    def wide(values, b, length):
+        value = values[:, b : b + 1].astype(jnp.float32)
+        return jnp.broadcast_to(value, (length, chans))
+
+    def put_middle(at, middle):
         for b in range(t_cols):
             mask[at, b * MB : (b + 1) * MB, :] = wide(middle, b, MB)
+
+    def put_sides(at, right, left):
         mask[at, cols : cols + EDGE, :] = wide(right, 0, EDGE)
         mask[at, cols + EDGE :, :] = wide(left, t_cols - 1, EDGE)
 
@@ -200,6 +209,23 @@
 
     def hide(row, value):
         h[row] = (value * mask[(row + MB - 1) // MB]).astype(h.dtype)
+
+    def hide_middle(row, value):
+        value = value * mask[(row + MB - 1) // MB, :cols]
+        h[row, :cols] = value.astype(h.dtype)
+
+    tile = 2 * EDGE
+    strip = ((cols - tile, tile), (cols, tile), (0, tile))
+    early = lax.broadcasted_iota(jnp.int32, (tile, chans), 0) < EDGE
+
+    def hide_strip(row, value):
+        for n, (start, length) in enumerate(strip):
+            at = pl.ds(start, length)
+            new = value[n * tile : (n + 1) * tile] * mask[(row + MB - 1) // MB, at]
+            if n != 1:
+                old = h[row, at].astype(jnp.float32)
+                new = jnp.where(early, *((old, new) if n == 0 else (new, old)))
+            h[row, at] = new.astype(h.dtype)
 
     def show(row, value):
         o[row] = (value[:cols] * mask[row // MB + 1, :cols]).astype(o.dtype)
@@ -208,22 +234,34 @@
         copy.wait()
     for copy in weights:
         copy.wait()
+    for t in range(t_rows):
+        put_middle(1 + t, tis[pl.ds(t, 1)])
+
+    inner1 = rows // 2 - 1
+    g1 = largest_divisor(inner1, 5)
+
+    def first_body(i, _):
+        firsts = [2 + 2 * (g1 * i + g) for g in range(g1)]
+        conv(x, firsts, w1, b1, hide_middle, ((0, cols),))
+        return 0
+
+    lax.fori_loop(0, inner1 // g1, first_body, 0)
+
     receive(False)
     for t in range(t_rows):
         at = pl.ds(t, 1)
-        put_mask(1 + t, tis[at], tiles[index[0, 1], at], tiles[index[0, -1], at])
-
-    inner1 = rows // 2 - 1
-    g1 = largest_divisor(inner1, 3)
-
-    def first_body(i, _):
-        conv(x, [2 + 2 * (g1 * i + g) for g in range(g1)], w1, b1, hide)
+        put_sides(1 + t, tiles[index[0, 1], at], tiles[index[0, -1], at])
+    g3 = largest_divisor(inner1, 15)
+
+    def strip_body(i, _):
+        firsts = [2 + 2 * (g3 * i + g) for g in range(g3)]
+        conv(x, firsts, w1, b1, hide_strip, strip)
         return 0
 
-    lax.fori_loop(0, inner1 // g1, first_body, 0)
+    lax.fori_loop(0, inner1 // g3, strip_body, 0)
 
     inner2 = rows // 2 - 2
-    g2 = largest_divisor(inner2, 3)
+    g2 = largest_divisor(inner2, 7)
 
     def second_body(i, _):
         conv(h, [2 + 2 * (g2 * i + g) for g in range(g2)], w2, b2, show)
@@ -233,7 +271,8 @@
 
     receive(True)
     for dr, at, t in ((-1, 0, t_rows - 1), (1, t_rows + 1, 0)):
-        put_mask(at, *[tiles[index[dr, dc], pl.ds(t, 1)] for dc in (0, 1, -1)])
+        put_middle(at, tiles[index[dr, 0], pl.ds(t, 1)])
+        put_sides(at, *[tiles[index[dr, dc], pl.ds(t, 1)] for dc in (1, -1)])
     conv(x, [0, rows], w1, b1, hide)
     for n, (dr, dc) in enumerate(AROUND):
 

time: 15 us -> 13.7 us (0.913)
  Pallas kernels: 14.8 us -> 13.5 us
    pallas_call x1, Pallas kernels: 13.5 us -> 12.1 us  [shards(): pl.pallas_call(functools.partial(inner_kernel, grid), out_shape=[pltpu.VM...]
where the time goes in v3:
time: 13.7 us; the launch traced here: 13.5 us
  Pallas kernels  13.5 us (99%)
    pallas_call x1, Pallas kernels, shards(): pl.pallas_call(functools.partial(inner_kernel, grid), out_shape=[pltpu.VM...  12.1 us
    pallas_call x1, Pallas kernels, shards(): pl.pallas_call(outer_kernel, out_shape=jax.ShapeDtypeStruct((rows, cols,...  1.39 us

profile of v3, /device:TPU:0, one launch (start us, length us, event | category | flops | bytes accessed | tf_op | source)
XLA Modules:
  0.0 13.5 jit_solution(2902717346028776525)
XLA Ops:
  0.0 12.1 %shard_map.64 = (bf16[34,272,128]{2,1,0:T(8,128)(2,1)S(1)}, bf16[32,256,128]{2,1,0:T(8,128)(2,1)S(1)}, bf16[4,3,128,256]{3,2,1,0:T(8,128)(2,1)S(1)}, f32[3,272,128]{2,1,0:T(8,128)S(1)}, f32[1,128]{1,0:T(1,128)S(1)}) custom-call(bf16[32,256,128]{2,1,0:T(8,128)(2,1)} %img.1, s32[1,8]{1,0:T(1,128)} %tis_in.1, bf16[3,3,128,128]{3,2,1,0:T(8,128)(2,1)} %k1.1, ...), custom_call_target="tpu_custom_call" | custom-call | tf_op jit(solution)/shard_map/pallas_call | solution.py:318
  12.1 1.4 %shard_map.65 = bf16[32,256,128]{2,1,0:T(8,128)(2,1)} custom-call(bf16[34,272,128]{2,1,0:T(8,128)(2,1)S(1)} %get-tuple-element.10.h, bf16[32,256,128]{2,1,0:T(8,128)(2,1)S(1)} %get-tuple-element.11.o, bf16[4,3,128,256]{3,2,1,0:T(8,128)(2,1)S(1)} %get-tuple-element.12.w2, f32[3,272,128]{2,1,0:T(8,128)S(1)} %get-tuple-element.13.mask, ...), custom_call_target="tpu_custom_call" | custom-call | tf_op jit(solution)/shard_map/pallas_call | solution.py:357
